TPU v7x, 256 devices: a 8x8x2 block of a 8x8x16 slice. The times are simulated.
256 devices in a mesh: grp: 2 (over z), row: 128 (over y, x, core).
Axes of the slice: x: 8, y: 8, z: 2, core: 2. Of those that a mesh axis runs over, the one named last changes fastest.
The devices are a block of a 8x8x16 slice.
Arguments:
- concentration: float32 [16, 1024, 1024], P('grp', 'row'), parts along dimension 0, may hold values from -0.95 to 1.35
- target_mass: float32 [16], P('grp'), parts along dimension 0, may hold values from 0 to 0.4
- mobility: float32 [16], P('grp'), parts along dimension 0, may hold values from 0.5 to 2
Outputs:
- updated: float32 [16, 1024, 1024], P('grp', 'row'), parts along dimension 0
- residual: float32 [16], P('grp'), parts along dimension 0
There are 2 independent parts, one for each index of `grp`. A program takes and returns all parts, laid end to end along the dimension named above; each array names one. Nothing has to cross between parts.
All inputs are finite; a program needn't handle non-finite values.
Results may differ from a plain program's by a relative error of at most 0.00005.
Values sent between devices are 32-bit elements; how exact they have to be, the bound alone decides.
A program may use at most 64 MiB of HBM per device.

v0:
```python
import math
import jax
import jax.numpy as jnp
from jax import lax
from jax.sharding import Mesh
from jax.sharding import PartitionSpec as P

ROW = ("row_0", "row_1", "row_2")
stiffness = 1.0
time_step = 0.05
stabilizer = 2.0


def by_axis(x, axes):
    for axis in axes:
        x = lax.psum(x, axis)
    return x


def make_tables(length):
    blocks = length // 128
    short_range = jnp.arange(blocks, dtype=jnp.int32)
    long_range = jnp.arange(128, dtype=jnp.int32)
    short_angle = (short_range[:, None] * short_range[None, :] % blocks).astype(jnp.float32) * (
        2.0 * math.pi / blocks
    )
    long_angle = (long_range[:, None] * long_range[None, :] % 128).astype(jnp.float32) * (
        2.0 * math.pi / 128
    )
    twist_angle = (short_range[:, None] * long_range[None, :]).astype(jnp.float32) * (
        2.0 * math.pi / length
    )
    return (
        jnp.cos(short_angle),
        jnp.sin(short_angle),
        jnp.cos(long_angle),
        jnp.sin(long_angle),
        jnp.cos(twist_angle),
        jnp.sin(twist_angle),
    )


def product(pattern, real_part, imag_part, cosine, sine, orient, real_only=False):

    def contract(operand, table):
        return jnp.einsum(pattern, operand, table, precision=lax.Precision.HIGHEST)

    if imag_part is None:
        return (contract(real_part, cosine), orient * contract(real_part, sine))
    if real_only:
        return (contract(real_part, cosine) - orient * contract(imag_part, sine), None)
    return (
        contract(real_part, cosine) - orient * contract(imag_part, sine),
        contract(imag_part, cosine) + orient * contract(real_part, sine),
    )


def rotate(real_part, imag_part, tables, orient):
    cosine, sine = (tables[4], tables[5])
    return (
        real_part * cosine - orient * imag_part * sine,
        imag_part * cosine + orient * real_part * sine,
    )


def forward_rows(real_field, tables, imag_field=None):
    planes, narrow, length = real_field.shape
    block_shape = (planes, narrow, length // 128, 128)
    shaped = real_field.reshape(block_shape)
    imag_shaped = None
    real_part, imag_part = product("pxab,ac->pxcb", shaped, imag_shaped, tables[0], tables[1], -1.0)
    real_part, imag_part = rotate(real_part, imag_part, tables, -1.0)
    real_part, imag_part = product(
        "pxcb,bd->pcdx", real_part, imag_part, tables[2], tables[3], -1.0
    )
    return (real_part.reshape(planes, length, narrow), imag_part.reshape(planes, length, narrow))


def forward_cols(pieces, tables):
    real_part, imag_part = pieces
    planes, narrow, length = real_part.shape
    shape = (planes, narrow, length // 128, 128)
    real_part, imag_part = product(
        "pqab,ac->pqcb",
        real_part.reshape(shape),
        imag_part.reshape(shape),
        tables[0],
        tables[1],
        -1.0,
    )
    real_part, imag_part = rotate(real_part, imag_part, tables, -1.0)
    real_part, imag_part = product(
        "pqcb,bd->pqcd", real_part, imag_part, tables[2], tables[3], -1.0
    )
    return (real_part.reshape(planes, narrow, length), imag_part.reshape(planes, narrow, length))


def inverse_cols(real_part, imag_part, tables):
    planes, narrow, length = real_part.shape
    shape = (planes, narrow, length // 128, 128)
    real_part, imag_part = product(
        "pqcd,db->pqcb",
        real_part.reshape(shape),
        imag_part.reshape(shape),
        tables[2],
        tables[3],
        1.0,
    )
    real_part, imag_part = rotate(real_part, imag_part, tables, 1.0)
    real_part, imag_part = product("pqcb,ca->pabq", real_part, imag_part, tables[0], tables[1], 1.0)
    return (real_part.reshape(planes, length, narrow), imag_part.reshape(planes, length, narrow))


def inverse_rows(pieces, tables):
    real_part, imag_part = pieces
    planes, narrow, length = real_part.shape
    shape = (planes, narrow, length // 128, 128)
    real_part, imag_part = product(
        "pxcd,db->pxcb",
        real_part.reshape(shape),
        imag_part.reshape(shape),
        tables[2],
        tables[3],
        1.0,
    )
    real_part, imag_part = rotate(real_part, imag_part, tables, 1.0)
    real_part, imag_part = product(
        "pxcb,ca->pxab", real_part, imag_part, tables[0], tables[1], 1.0, True
    )
    real_part = real_part.reshape(planes, narrow, length)
    return real_part


def digit_natural(positions, length):
    blocks = length // 128
    return positions // 128 + blocks * (positions % 128)


def wavenumbers(natural_index, length):
    signed = jnp.where(natural_index < length // 2, natural_index, natural_index - length)
    angular = signed.astype(jnp.float32) * (2.0 * math.pi / length)
    return (angular, jnp.where(natural_index == length // 2, jnp.float32(0.0), angular))


def local(concentration, target_mass, mobility):
    planes, rows_local, width_y = concentration.shape
    devices = lax.axis_size(ROW)
    width_x = rows_local * devices
    cols_local = width_y // devices
    cells = float(width_x * width_y)
    inverse_cells = 1.0 / cells
    residual = by_axis(jnp.sum(concentration, axis=(1, 2)), ROW) / cells - target_mass
    tables_y = make_tables(width_y)
    device = lax.axis_index(ROW)
    local_slots = jnp.arange(cols_local, dtype=jnp.int32)
    columns = device * cols_local + local_slots
    all_x = jnp.arange(width_x, dtype=jnp.int32)
    natural_x = digit_natural(all_x, width_x)
    angular_x, slope_x = wavenumbers(natural_x, width_x)
    angular_x, slope_x = (angular_x[None, :], slope_x[None, :])
    cubic_term = concentration * concentration * concentration - concentration

    def to_spectrum(pieces):
        return forward_cols(pieces, tables_y)

    angular_y, slope_y = wavenumbers(digit_natural(columns, width_y), width_y)
    stacked = jnp.concatenate([concentration, cubic_term], axis=0)
    half_real, half_imag = forward_rows(stacked, tables_y)
    spec_real, spec_imag = to_spectrum(
        (
            lax.all_to_all(half_real, ROW, split_axis=1, concat_axis=2, tiled=True),
            lax.all_to_all(half_imag, ROW, split_axis=1, concat_axis=2, tiled=True),
        )
    )
    field_real, field_imag = (spec_real[:planes], spec_imag[:planes])
    cubic_real, cubic_imag = (spec_real[planes:], spec_imag[planes:])
    angular_y, slope_y = (angular_y[:, None], slope_y[:, None])
    square = angular_x * angular_x + angular_y * angular_y
    chem_real = (cubic_real + stiffness * square * field_real) * inverse_cells
    chem_imag = (cubic_imag + stiffness * square * field_imag) * inverse_cells
    stack_real = jnp.concatenate([-slope_x * chem_imag, -slope_y * chem_imag], axis=0)
    stack_imag = jnp.concatenate([slope_x * chem_real, slope_y * chem_real], axis=0)
    back_real, back_imag = inverse_cols(stack_real, stack_imag, tables_y)
    gradient_pair = inverse_rows(
        (
            lax.all_to_all(back_real, ROW, split_axis=1, concat_axis=2, tiled=True),
            lax.all_to_all(back_imag, ROW, split_axis=1, concat_axis=2, tiled=True),
        ),
        tables_y,
    )
    grad_x = gradient_pair[:planes]
    grad_y = gradient_pair[planes:]
    weight = mobility[:, None, None] / (1.0 + concentration * concentration)
    fluxes = jnp.concatenate([weight * grad_x, weight * grad_y], axis=0)
    flux_half_real, flux_half_imag = forward_rows(fluxes, tables_y)
    flux_real, flux_imag = to_spectrum(
        (
            lax.all_to_all(flux_half_real, ROW, split_axis=1, concat_axis=2, tiled=True),
            lax.all_to_all(flux_half_imag, ROW, split_axis=1, concat_axis=2, tiled=True),
        )
    )
    flux_x_real, flux_x_imag = (flux_real[:planes], flux_imag[:planes])
    flux_y_real, flux_y_imag = (flux_real[planes:], flux_imag[planes:])
    div_real = -slope_x * flux_x_imag - slope_y * flux_y_imag
    div_imag = slope_x * flux_x_real + slope_y * flux_y_real
    factor = (
        time_step
        * inverse_cells
        / (
            1.0
            + time_step
            * mobility[:, None, None]
            * (stabilizer * square + stiffness * square * square)
        )
    )
    change_real, change_imag = inverse_cols(div_real * factor, div_imag * factor, tables_y)
    change = inverse_rows(
        (
            lax.all_to_all(change_real, ROW, split_axis=1, concat_axis=2, tiled=True),
            lax.all_to_all(change_imag, ROW, split_axis=1, concat_axis=2, tiled=True),
        ),
        tables_y,
    )
    fresh = concentration + change
    return (fresh - residual[:, None, None], residual)


def solution(mesh):
    torus = Mesh(
        mesh.devices.reshape(mesh.shape["grp"], 8, 8, 2), ("grp", "row_0", "row_1", "row_2")
    )
    in_specs = (P("grp", ROW, None), P("grp"), P("grp"))
    out_specs = (P("grp", ROW, None), P("grp"))
    return jax.shard_map(local, mesh=torus, in_specs=in_specs, out_specs=out_specs, check_vma=False)
```

profile of v0, /device:TPU:513, one launch (start us, length us, event | category | flops | bytes accessed | tf_op | source)
XLA Modules:
  0.0 410.4 jit_solution(5268577525299020385)
XLA Ops:
  6.6 2.7 copy.114
  9.3 4.2 %reshape.381 = f32[128,1,1024]{2,1,0:T(1,128)} reshape(f32[1024,8,16]{2,1,0:T(8,128)} %bitcast.296) | data formatting | bytes 1048576
  13.5 28.1 %all-to-all-start.1 = ((f32[128,1,1024]{2,1,0:T(1,128)}), f32[128,1,1024]{2,1,0:T(1,128)S(1)}, u32[]{:S(2)}, u32[]{:S(2)}) async-start(f32[128,1,1024]{2,1,0:T(1,128)} %reshape.381), calls=%async_computation.1 | async-start | bytes 1048576 | tf_op jit(solution)/shard_map/all_to_all | solution.py:171
  43.9 2.7 copy.108
  46.6 4.2 %reshape.383 = f32[128,1,1024]{2,1,0:T(1,128)} reshape(f32[1024,8,16]{2,1,0:T(8,128)} %bitcast.297) | data formatting | bytes 1048576
  50.8 10.3 %all-to-all-done.1 = f32[128,1,1024]{2,1,0:T(1,128)S(1)} async-done(((f32[128,1,1024]{2,1,0:T(1,128)}), f32[128,1,1024]{2,1,0:T(1,128)S(1)}, u32[]{:S(2)}, u32[]{:S(2)}) %all-to-all-start.1) | async-done | bytes 524320 | tf_op jit(solution)/shard_map/all_to_all | solution.py:171
  61.0 7.5 %all-to-all-start = ((f32[128,1,1024]{2,1,0:T(1,128)}), f32[128,1,1024]{2,1,0:T(1,128)S(1)}, u32[]{:S(2)}, u32[]{:S(2)}) async-start(f32[128,1,1024]{2,1,0:T(1,128)} %reshape.383), calls=%async_computation | async-start | bytes 1048576 | tf_op jit(solution)/shard_map/all_to_all | solution.py:172
  71.1 2.8 reshape.382
  73.9 4.4 %copy.115 = f32[16,8,128,8]{0,3,2,1:T(8,128)} copy(f32[16,8,128,8]{0,3,1,2:T(8,128)} %bitcast.302) | data formatting | bytes 1048576 | tf_op jit(solution)/shard_map/all_to_all | solution.py:171
  78.3 2.9 copy.116
  81.8 6.3 %all-to-all-done = f32[128,1,1024]{2,1,0:T(1,128)S(1)} async-done(((f32[128,1,1024]{2,1,0:T(1,128)}), f32[128,1,1024]{2,1,0:T(1,128)S(1)}, u32[]{:S(2)}, u32[]{:S(2)}) %all-to-all-start) | async-done | bytes 524320 | tf_op jit(solution)/shard_map/all_to_all | solution.py:172
  88.1 1.9 reduce
  90.0 2.8 reshape.384
  92.7 4.4 %copy.109 = f32[16,8,128,8]{0,3,2,1:T(8,128)} copy(f32[16,8,128,8]{0,3,1,2:T(8,128)} %bitcast.304) | data formatting | bytes 1048576 | tf_op jit(solution)/shard_map/all_to_all | solution.py:172
  97.2 3.3 copy.110
  110.4 3.1 copy.159
  113.5 4.2 %reshape.387 = f32[128,1,1024]{2,1,0:T(1,128)} reshape(f32[1024,8,16]{2,1,0:T(8,128)} %bitcast.298) | data formatting | bytes 1048576
  117.7 10.1 %all-to-all-start.2 = ((f32[128,1,1024]{2,1,0:T(1,128)}), f32[128,1,1024]{2,1,0:T(1,128)S(1)}, u32[]{:S(2)}, u32[]{:S(2)}) async-start(f32[128,1,1024]{2,1,0:T(1,128)} %reshape.387), calls=%async_computation.2 | async-start | bytes 1048576 | tf_op jit(solution)/shard_map/all_to_all | solution.py:186
  129.0 3.1 copy.160
  132.1 4.2 %reshape.385 = f32[128,1,1024]{2,1,0:T(1,128)} reshape(f32[1024,8,16]{2,1,0:T(8,128)} %bitcast.299) | data formatting | bytes 1048576
  136.3 11.1 %all-to-all-done.2 = f32[128,1,1024]{2,1,0:T(1,128)S(1)} async-done(((f32[128,1,1024]{2,1,0:T(1,128)}), f32[128,1,1024]{2,1,0:T(1,128)S(1)}, u32[]{:S(2)}, u32[]{:S(2)}) %all-to-all-start.2) | async-done | bytes 524320 | tf_op jit(solution)/shard_map/all_to_all | solution.py:186
  147.4 7.5 %all-to-all-start.3 = ((f32[128,1,1024]{2,1,0:T(1,128)}), f32[128,1,1024]{2,1,0:T(1,128)S(1)}, u32[]{:S(2)}, u32[]{:S(2)}) async-start(f32[128,1,1024]{2,1,0:T(1,128)} %reshape.385), calls=%async_computation.3 | async-start | bytes 1048576 | tf_op jit(solution)/shard_map/all_to_all | solution.py:187
  154.9 1.9 reduce.3
  156.8 2.9 reshape.388
  159.8 2.5 copy.120
  162.2 6.7 %fusion.104 = f32[16,8,8,128]{3,0,2,1:T(8,128)S(1)} fusion(f32[16,8,8,128]{0,3,2,1:T(8,128)S(1)} %bitcast.292), kind=kOutput, calls=%fused_computation.167 | convolution fusion | flops 201555968 | bytes 1048576 | tf_op jit(solution)/shard_map/pxcd,db->pxcb/dot_general | solution.py:46
  168.9 6.7 %fusion.128 = f32[16,8,8,128]{3,0,2,1:T(8,128)S(1)} fusion(f32[16,8,8,128]{0,3,2,1:T(8,128)S(1)} %bitcast.293), kind=kOutput, calls=%fused_computation.191 | convolution fusion | flops 201555968 | bytes 1048576 | tf_op jit(solution)/shard_map/pxcd,db->pxcb/dot_general | solution.py:46
  175.6 1.9 reduce.2
  177.5 3.1 reshape.386
  180.7 2.5 copy.123
  183.1 6.7 %fusion.106 = f32[16,8,8,128]{3,0,2,1:T(8,128)S(1)} fusion(f32[16,8,8,128]{0,3,2,1:T(8,128)S(1)} %bitcast.294), kind=kOutput, calls=%fused_computation.169 | convolution fusion | flops 201555968 | bytes 1048576 | tf_op jit(solution)/shard_map/pxcd,db->pxcb/dot_general | solution.py:46
  189.8 6.7 %fusion.126 = f32[16,8,8,128]{3,0,2,1:T(8,128)S(1)} fusion(f32[16,8,8,128]{0,3,2,1:T(8,128)S(1)} %bitcast.295), kind=kOutput, calls=%fused_computation.189 | convolution fusion | flops 201555968 | bytes 1048576 | tf_op jit(solution)/shard_map/pxcd,db->pxcb/dot_general | solution.py:46
  203.8 2.7 copy.140
  206.5 4.2 %reshape.389 = f32[128,1,1024]{2,1,0:T(1,128)} reshape(f32[1024,8,16]{2,1,0:T(8,128)} %bitcast.300) | data formatting | bytes 1048576
  210.7 17.1 %all-to-all-start.5 = ((f32[128,1,1024]{2,1,0:T(1,128)}), f32[128,1,1024]{2,1,0:T(1,128)S(1)}, u32[]{:S(2)}, u32[]{:S(2)}) async-start(f32[128,1,1024]{2,1,0:T(1,128)} %reshape.389), calls=%async_computation.5 | async-start | bytes 1048576 | tf_op jit(solution)/shard_map/all_to_all | solution.py:198
  230.1 2.7 copy.134
  232.9 4.2 %reshape.391 = f32[128,1,1024]{2,1,0:T(1,128)} reshape(f32[1024,8,16]{2,1,0:T(8,128)} %bitcast.301) | data formatting | bytes 1048576
  237.0 9.9 %all-to-all-done.5 = f32[128,1,1024]{2,1,0:T(1,128)S(1)} async-done(((f32[128,1,1024]{2,1,0:T(1,128)}), f32[128,1,1024]{2,1,0:T(1,128)S(1)}, u32[]{:S(2)}, u32[]{:S(2)}) %all-to-all-start.5) | async-done | bytes 524320 | tf_op jit(solution)/shard_map/all_to_all | solution.py:198
  247.0 7.5 %all-to-all-start.4 = ((f32[128,1,1024]{2,1,0:T(1,128)}), f32[128,1,1024]{2,1,0:T(1,128)S(1)}, u32[]{:S(2)}, u32[]{:S(2)}) async-start(f32[128,1,1024]{2,1,0:T(1,128)} %reshape.391), calls=%async_computation.4 | async-start | bytes 1048576 | tf_op jit(solution)/shard_map/all_to_all | solution.py:199
  254.5 1.9 reduce.5
  256.4 2.8 reshape.390
  259.1 4.4 %copy.141 = f32[16,8,128,8]{0,3,2,1:T(8,128)} copy(f32[16,8,128,8]{0,3,1,2:T(8,128)} %bitcast.308) | data formatting | bytes 1048576 | tf_op jit(solution)/shard_map/all_to_all | solution.py:198
  263.6 2.9 copy.142
  267.0 7.0 %all-to-all-done.4 = f32[128,1,1024]{2,1,0:T(1,128)S(1)} async-done(((f32[128,1,1024]{2,1,0:T(1,128)}), f32[128,1,1024]{2,1,0:T(1,128)S(1)}, u32[]{:S(2)}, u32[]{:S(2)}) %all-to-all-start.4) | async-done | bytes 524320 | tf_op jit(solution)/shard_map/all_to_all | solution.py:199
  274.0 1.9 reduce.4
  275.9 2.8 reshape.392
  278.7 4.4 %copy.135 = f32[16,8,128,8]{0,3,2,1:T(8,128)} copy(f32[16,8,128,8]{0,3,1,2:T(8,128)} %bitcast.310) | data formatting | bytes 1048576 | tf_op jit(solution)/shard_map/all_to_all | solution.py:199
  283.1 3.0 copy.136
  294.8 3.1 copy.161
  297.9 4.5 %reshape.395 = f32[128,1,512]{2,1,0:T(1,128)} reshape(f32[1024,8,8]{2,1,0:T(8,128)} %bitcast.312) | data formatting | bytes 524288
  302.4 9.3 %all-to-all-start.6 = ((f32[128,1,512]{2,1,0:T(1,128)}), f32[128,1,512]{2,1,0:T(1,128)S(1)}, u32[]{:S(2)}, u32[]{:S(2)}) async-start(f32[128,1,512]{2,1,0:T(1,128)} %reshape.395), calls=%async_computation.6 | async-start | bytes 524288 | tf_op jit(solution)/shard_map/all_to_all | solution.py:219
  312.5 3.1 copy.164
  315.6 4.5 %reshape.393 = f32[128,1,512]{2,1,0:T(1,128)} reshape(f32[1024,8,8]{2,1,0:T(8,128)} %bitcast.313) | data formatting | bytes 524288
  320.1 5.9 %all-to-all-done.6 = f32[128,1,512]{2,1,0:T(1,128)S(1)} async-done(((f32[128,1,512]{2,1,0:T(1,128)}), f32[128,1,512]{2,1,0:T(1,128)S(1)}, u32[]{:S(2)}, u32[]{:S(2)}) %all-to-all-start.6) | async-done | bytes 262176 | tf_op jit(solution)/shard_map/all_to_all | solution.py:219
  326.0 10.4 %all-to-all-start.7 = ((f32[128,1,512]{2,1,0:T(1,128)}), f32[128,1,512]{2,1,0:T(1,128)S(1)}, u32[]{:S(2)}, u32[]{:S(2)}) async-start(f32[128,1,512]{2,1,0:T(1,128)} %reshape.393), calls=%async_computation.7 | async-start | bytes 524288 | tf_op jit(solution)/shard_map/all_to_all | solution.py:220
  336.4 16.2 %psum.21 = f32[8]{0:T(128)S(1)} all-reduce(f32[8]{0:T(128)S(1)} %get-tuple-element.14), channel_id=1, replica_groups=mesh['grp'=2,'row_0'=8,'row_1'=8,'row_2'=2] {'row_0'}, use_global_device_ids=true, to_apply=%region_1.0 | all-reduce | flops 8 | bytes 64 | tf_op jit(solution)/shard_map/psum | solution.py:16
  352.6 12.9 %psum.22 = f32[8]{0:T(128)S(1)} all-reduce(f32[8]{0:T(128)S(1)} %psum.21), channel_id=1, replica_groups=mesh['grp'=2,'row_0'=8,'row_1'=8,'row_2'=2] {'row_1'}, use_global_device_ids=true, to_apply=%region_2.0 | all-reduce | flops 8 | bytes 64 | tf_op jit(solution)/shard_map/psum | solution.py:16
  365.5 9.7 %psum.23 = f32[8]{0:T(128)S(1)} all-reduce(f32[8]{0:T(128)S(1)} %psum.22), channel_id=1, replica_groups=mesh['grp'=2,'row_0'=8,'row_1'=8,'row_2'=2] {'row_2'}, use_global_device_ids=true, to_apply=%region_3.0 | all-reduce | flops 8 | bytes 64 | tf_op jit(solution)/shard_map/psum | solution.py:16
  376.5 3.6 reshape.396
  380.1 6.6 %copy.147 = f32[8,8,128,8]{3,2,1,0:T(8,128)} copy(f32[8,8,128,8]{3,0,1,2:T(8,128)} %bitcast.314) | data formatting | bytes 524288 | tf_op jit(solution)/shard_map/all_to_all | solution.py:219
  386.7 3.6 reshape.373
  392.2 3.6 reshape.394
  395.8 6.6 %copy.150 = f32[8,8,128,8]{3,2,1,0:T(8,128)} copy(f32[8,8,128,8]{3,0,1,2:T(8,128)} %bitcast.315) | data formatting | bytes 524288 | tf_op jit(solution)/shard_map/all_to_all | solution.py:220
  402.4 3.9 reshape.375
  (91 shorter events, 48.6 us)
Async XLA Ops:
  13.5 47.6 %all-to-all-start.1 = ((f32[128,1,1024]{2,1,0:T(1,128)}), f32[128,1,1024]{2,1,0:T(1,128)S(1)}, u32[]{:S(2)}, u32[]{:S(2)}) async-start(f32[128,1,1024]{2,1,0:T(1,128)} %reshape.381), calls=%async_computation.1 | async-start | bytes 1048576 | tf_op jit(solution)/shard_map/all_to_all | solution.py:171
  61.0 27.1 %all-to-all-start = ((f32[128,1,1024]{2,1,0:T(1,128)}), f32[128,1,1024]{2,1,0:T(1,128)S(1)}, u32[]{:S(2)}, u32[]{:S(2)}) async-start(f32[128,1,1024]{2,1,0:T(1,128)} %reshape.383), calls=%async_computation | async-start | bytes 1048576 | tf_op jit(solution)/shard_map/all_to_all | solution.py:172
  117.7 29.7 %all-to-all-start.2 = ((f32[128,1,1024]{2,1,0:T(1,128)}), f32[128,1,1024]{2,1,0:T(1,128)S(1)}, u32[]{:S(2)}, u32[]{:S(2)}) async-start(f32[128,1,1024]{2,1,0:T(1,128)} %reshape.387), calls=%async_computation.2 | async-start | bytes 1048576 | tf_op jit(solution)/shard_map/all_to_all | solution.py:186
  147.4 28.2 %all-to-all-start.3 = ((f32[128,1,1024]{2,1,0:T(1,128)}), f32[128,1,1024]{2,1,0:T(1,128)S(1)}, u32[]{:S(2)}, u32[]{:S(2)}) async-start(f32[128,1,1024]{2,1,0:T(1,128)} %reshape.385), calls=%async_computation.3 | async-start | bytes 1048576 | tf_op jit(solution)/shard_map/all_to_all | solution.py:187
  196.5 3.4 copy-start
  196.5 3.4 copy-start.1
  210.7 36.3 %all-to-all-start.5 = ((f32[128,1,1024]{2,1,0:T(1,128)}), f32[128,1,1024]{2,1,0:T(1,128)S(1)}, u32[]{:S(2)}, u32[]{:S(2)}) async-start(f32[128,1,1024]{2,1,0:T(1,128)} %reshape.389), calls=%async_computation.5 | async-start | bytes 1048576 | tf_op jit(solution)/shard_map/all_to_all | solution.py:198
  247.0 27.1 %all-to-all-start.4 = ((f32[128,1,1024]{2,1,0:T(1,128)}), f32[128,1,1024]{2,1,0:T(1,128)S(1)}, u32[]{:S(2)}, u32[]{:S(2)}) async-start(f32[128,1,1024]{2,1,0:T(1,128)} %reshape.391), calls=%async_computation.4 | async-start | bytes 1048576 | tf_op jit(solution)/shard_map/all_to_all | solution.py:199
  302.4 23.6 %all-to-all-start.6 = ((f32[128,1,512]{2,1,0:T(1,128)}), f32[128,1,512]{2,1,0:T(1,128)S(1)}, u32[]{:S(2)}, u32[]{:S(2)}) async-start(f32[128,1,512]{2,1,0:T(1,128)} %reshape.395), calls=%async_computation.6 | async-start | bytes 524288 | tf_op jit(solution)/shard_map/all_to_all | solution.py:219
  312.5 62.7 %copy-start.3 = (f32[8]{0:T(128)S(1)}, f32[8]{0:T(128)}, u32[]{:S(2)}) copy-start(f32[8]{0:T(128)} %param.4) | copy-start | bytes 100
  326.0 64.9 %all-to-all-start.7 = ((f32[128,1,512]{2,1,0:T(1,128)}), f32[128,1,512]{2,1,0:T(1,128)S(1)}, u32[]{:S(2)}, u32[]{:S(2)}) async-start(f32[128,1,512]{2,1,0:T(1,128)} %reshape.393), calls=%async_computation.7 | async-start | bytes 524288 | tf_op jit(solution)/shard_map/all_to_all | solution.py:220
  375.2 33.9 %copy-start.2 = (f32[8]{0:T(128)}, f32[8]{0:T(128)S(1)}, u32[]{:S(2)}) copy-start(f32[8]{0:T(128)S(1)} %multiply_subtract_fusion.13) | copy-start | bytes 100
where the time goes:
time: 418 us; the launch traced here: 410 us
  local copies, waits for them, and re-layouts  139 us (33%)
  starting transfers between devices  97.4 us (23%)
  matrix products  65.4 us (16%)
  waiting for transfers between devices  50.5 us (12%)
  blocking collectives  38.8 us (9%)
  other arithmetic  17.4 us (4%)
    dot_general x56, matrix products, contract(): return jnp.einsum(pattern, operand, table, precision=lax.Precision.HIGHEST)  65.4 us
    unnamed x24, local copies, waits for them, and re-layouts  58.3 us
    psum x3, blocking collectives, by_axis(): x = lax.psum(x, axis)  38.8 us
    all_to_all x1, starting transfers between devices, local(): lax.all_to_all(half_real, ROW, split_axis=1, concat_axis=2, tiled=True)  28.1 us
    all_to_all x1, starting transfers between devices, local(): lax.all_to_all(flux_half_real, ROW, split_axis=1, concat_axis=2, tiled=True)  17.1 us
    all_to_all x1, waiting for transfers between devices, local(): lax.all_to_all(back_real, ROW, split_axis=1, concat_axis=2, tiled=True)  11.1 us
    all_to_all x1, starting transfers between devices, local(): lax.all_to_all(change_imag, ROW, split_axis=1, concat_axis=2, tiled=True)  10.4 us
    all_to_all x1, waiting for transfers between devices, local(): lax.all_to_all(half_real, ROW, split_axis=1, concat_axis=2, tiled=True)  10.3 us
  transfers between devices with their start and end apart: 8, of which 6 were waited for; matrix products, arithmetic and copies ran while one was open for 24% of the time, Pallas kernels for 0%

commit v1 on v0

--- a/solution.py
+++ b/solution.py
@@ -168,7 +168,12 @@
     half_real, half_imag = forward_rows(stacked, tables_y)
     spec_real, spec_imag = to_spectrum(
         (
-            lax.all_to_all(half_real, ROW, split_axis=1, concat_axis=2, tiled=True),
+            jnp.concatenate(
+                lax.all_to_all(
+                    jnp.stack(jnp.split(half_real, lax.axis_size(ROW), axis=1)), ROW, 0, 0
+                ),
+                axis=2,
+            ),
             lax.all_to_all(half_imag, ROW, split_axis=1, concat_axis=2, tiled=True),
         )
     )

time: 418 us -> 521 us (1.25)
  local copies, waits for them, and re-layouts: 139 us -> 241 us
    unnamed x24 -> x151, local copies, waits for them, and re-layouts: 58.3 us -> 147 us
    another operation x0 -> x3, local copies, waits for them, and re-layouts: none -> 10.4 us  [the longest x2 7.54 us: local(): jnp.stack(jnp.split(half_real, lax.axis_size(ROW), axis=1))]
    reshape x2, local copies, waits for them, and re-layouts: 6.34 us -> 14.6 us  [forward_cols(): imag_part.reshape(shape)]
  transfers between devices with their start and end apart: 8 -> 8, of which waited for: 6 -> 6; matrix products, arithmetic and copies ran while one was open for 24% -> 19% of each run, Pallas kernels for 0% -> 0%
where the time goes in v1:
time: 521 us; the launch traced here: 513 us
  local copies, waits for them, and re-layouts  241 us (46%)
  starting transfers between devices  97.4 us (19%)
  matrix products  65.4 us (13%)
  waiting for transfers between devices  50.6 us (10%)
  blocking collectives  38.8 us (7%)
  other arithmetic  17.4 us (3%)
    unnamed x151, local copies, waits for them, and re-layouts  147 us
    dot_general x56, matrix products, contract(): return jnp.einsum(pattern, operand, table, precision=lax.Precision.HIGHEST)  65.4 us
    psum x3, blocking collectives, by_axis(): x = lax.psum(x, axis)  38.8 us
    all_to_all x1, starting transfers between devices, local(): lax.all_to_all(jnp.stack(jnp.split(half_real, lax.axis_size(ROW), axis=1)...  27.7 us
    all_to_all x1, starting transfers between devices, local(): lax.all_to_all(flux_half_real, ROW, split_axis=1, concat_axis=2, tiled=True)  17.1 us
    reshape x2, local copies, waits for them, and re-layouts, forward_cols(): imag_part.reshape(shape)  14.6 us
    all_to_all x1, waiting for transfers between devices, local(): lax.all_to_all(back_real, ROW, split_axis=1, concat_axis=2, tiled=True)  11.1 us
    all_to_all x1, waiting for transfers between devices, local(): lax.all_to_all(jnp.stack(jnp.split(half_real, lax.axis_size(ROW), axis=1)...  10.6 us
  transfers between devices with their start and end apart: 8, of which 6 were waited for; matrix products, arithmetic and copies ran while one was open for 19% of the time, Pallas kernels for 0%

profile of v1, /device:TPU:513, one launch (start us, length us, event | category | flops | bytes accessed | tf_op | source)
XLA Modules:
  0.0 512.5 jit_solution(2314567108999219435)
XLA Ops:
  95.9 6.8 %copy.541 = f32[128,16,8,8]{1,3,2,0:T(8,128)} copy(f32[128,16,8,8]{2,3,1,0:T(8,128)} %constant_dynamic-update-slice_fusion) | data formatting | bytes 1048576 | tf_op jit(solution)/shard_map/stack | solution.py:173
  102.8 4.2 reshape.380
  106.9 27.7 %all-to-all-start.1 = ((f32[128,1,1024]{2,1,0:T(1,128)}), f32[128,1,1024]{2,1,0:T(1,128)S(1)}, u32[]{:S(2)}, u32[]{:S(2)}) async-start(f32[128,1,1024]{2,1,0:T(1,128)} %reshape.380), calls=%async_computation.1 | async-start | bytes 1048576 | tf_op jit(solution)/shard_map/all_to_all | solution.py:172
  137.0 2.7 copy.535
  139.7 4.2 reshape.382
  143.9 10.6 %all-to-all-done.1 = f32[128,1,1024]{2,1,0:T(1,128)S(1)} async-done(((f32[128,1,1024]{2,1,0:T(1,128)}), f32[128,1,1024]{2,1,0:T(1,128)S(1)}, u32[]{:S(2)}, u32[]{:S(2)}) %all-to-all-start.1) | async-done | bytes 524320 | tf_op jit(solution)/shard_map/all_to_all | solution.py:172
  154.5 7.5 %all-to-all-start = ((f32[128,1,1024]{2,1,0:T(1,128)}), f32[128,1,1024]{2,1,0:T(1,128)S(1)}, u32[]{:S(2)}, u32[]{:S(2)}) async-start(f32[128,1,1024]{2,1,0:T(1,128)} %reshape.382), calls=%async_computation | async-start | bytes 1048576 | tf_op jit(solution)/shard_map/all_to_all | solution.py:177
  164.6 2.8 reshape.381
  167.4 2.5 bitcast_bitcast_fusion
  169.9 2.2 copy.542
  172.1 2.9 copy.543
  175.5 6.1 %all-to-all-done = f32[128,1,1024]{2,1,0:T(1,128)S(1)} async-done(((f32[128,1,1024]{2,1,0:T(1,128)}), f32[128,1,1024]{2,1,0:T(1,128)S(1)}, u32[]{:S(2)}, u32[]{:S(2)}) %all-to-all-start) | async-done | bytes 524320 | tf_op jit(solution)/shard_map/all_to_all | solution.py:177
  181.6 1.9 reduce
  183.5 2.8 reshape.383
  186.3 4.4 copy.536
  190.7 11.6 %copy.537 = f32[16,8,8,128]{3,2,1,0:T(8,128)S(1)} copy(f32[16,8,8,128]{0,3,2,1:T(8,128)} %bitcast.944) | data formatting | bytes 1048576 | tf_op jit(solution)/shard_map/reshape | solution.py:86
  212.2 3.1 copy.586
  215.3 4.2 reshape.386
  219.5 10.4 %all-to-all-start.2 = ((f32[128,1,1024]{2,1,0:T(1,128)}), f32[128,1,1024]{2,1,0:T(1,128)S(1)}, u32[]{:S(2)}, u32[]{:S(2)}) async-start(f32[128,1,1024]{2,1,0:T(1,128)} %reshape.386), calls=%async_computation.2 | async-start | bytes 1048576 | tf_op jit(solution)/shard_map/all_to_all | solution.py:191
  231.1 3.1 copy.587
  234.2 4.2 reshape.384
  238.4 11.1 %all-to-all-done.2 = f32[128,1,1024]{2,1,0:T(1,128)S(1)} async-done(((f32[128,1,1024]{2,1,0:T(1,128)}), f32[128,1,1024]{2,1,0:T(1,128)S(1)}, u32[]{:S(2)}, u32[]{:S(2)}) %all-to-all-start.2) | async-done | bytes 524320 | tf_op jit(solution)/shard_map/all_to_all | solution.py:191
  249.4 7.5 %all-to-all-start.3 = ((f32[128,1,1024]{2,1,0:T(1,128)}), f32[128,1,1024]{2,1,0:T(1,128)S(1)}, u32[]{:S(2)}, u32[]{:S(2)}) async-start(f32[128,1,1024]{2,1,0:T(1,128)} %reshape.384), calls=%async_computation.3 | async-start | bytes 1048576 | tf_op jit(solution)/shard_map/all_to_all | solution.py:192
  257.0 1.9 reduce.3
  258.9 3.1 reshape.387
  262.0 2.5 copy.547
  264.5 6.7 %fusion.104 = f32[16,8,8,128]{3,0,2,1:T(8,128)S(1)} fusion(f32[16,8,8,128]{0,3,2,1:T(8,128)S(1)} %bitcast.932), kind=kOutput, calls=%fused_computation.423 | convolution fusion | flops 201555968 | bytes 1048576 | tf_op jit(solution)/shard_map/pxcd,db->pxcb/dot_general | solution.py:46
  271.1 6.7 %fusion.128 = f32[16,8,8,128]{3,0,2,1:T(8,128)S(1)} fusion(f32[16,8,8,128]{0,3,2,1:T(8,128)S(1)} %bitcast.933), kind=kOutput, calls=%fused_computation.447 | convolution fusion | flops 201555968 | bytes 1048576 | tf_op jit(solution)/shard_map/pxcd,db->pxcb/dot_general | solution.py:46
  277.9 1.9 reduce.2
  279.7 2.9 reshape.385
  282.7 2.5 copy.550
  285.1 6.7 %fusion.106 = f32[16,8,8,128]{3,0,2,1:T(8,128)S(1)} fusion(f32[16,8,8,128]{0,3,2,1:T(8,128)S(1)} %bitcast.934), kind=kOutput, calls=%fused_computation.425 | convolution fusion | flops 201555968 | bytes 1048576 | tf_op jit(solution)/shard_map/pxcd,db->pxcb/dot_general | solution.py:46
  291.9 6.7 %fusion.126 = f32[16,8,8,128]{3,0,2,1:T(8,128)S(1)} fusion(f32[16,8,8,128]{0,3,2,1:T(8,128)S(1)} %bitcast.935), kind=kOutput, calls=%fused_computation.445 | convolution fusion | flops 201555968 | bytes 1048576 | tf_op jit(solution)/shard_map/pxcd,db->pxcb/dot_general | solution.py:46
  305.9 2.7 copy.567
  308.6 4.2 reshape.388
  312.8 17.1 %all-to-all-start.5 = ((f32[128,1,1024]{2,1,0:T(1,128)}), f32[128,1,1024]{2,1,0:T(1,128)S(1)}, u32[]{:S(2)}, u32[]{:S(2)}) async-start(f32[128,1,1024]{2,1,0:T(1,128)} %reshape.388), calls=%async_computation.5 | async-start | bytes 1048576 | tf_op jit(solution)/shard_map/all_to_all | solution.py:203
  332.3 2.7 copy.561
  335.0 4.2 reshape.390
  339.2 9.9 %all-to-all-done.5 = f32[128,1,1024]{2,1,0:T(1,128)S(1)} async-done(((f32[128,1,1024]{2,1,0:T(1,128)}), f32[128,1,1024]{2,1,0:T(1,128)S(1)}, u32[]{:S(2)}, u32[]{:S(2)}) %all-to-all-start.5) | async-done | bytes 524320 | tf_op jit(solution)/shard_map/all_to_all | solution.py:203
  349.1 7.5 %all-to-all-start.4 = ((f32[128,1,1024]{2,1,0:T(1,128)}), f32[128,1,1024]{2,1,0:T(1,128)S(1)}, u32[]{:S(2)}, u32[]{:S(2)}) async-start(f32[128,1,1024]{2,1,0:T(1,128)} %reshape.390), calls=%async_computation.4 | async-start | bytes 1048576 | tf_op jit(solution)/shard_map/all_to_all | solution.py:204
  356.6 1.9 reduce.5
  358.5 2.8 reshape.389
  361.3 4.4 copy.568
  365.7 2.9 copy.569
  369.2 7.0 %all-to-all-done.4 = f32[128,1,1024]{2,1,0:T(1,128)S(1)} async-done(((f32[128,1,1024]{2,1,0:T(1,128)}), f32[128,1,1024]{2,1,0:T(1,128)S(1)}, u32[]{:S(2)}, u32[]{:S(2)}) %all-to-all-start.4) | async-done | bytes 524320 | tf_op jit(solution)/shard_map/all_to_all | solution.py:204
  378.0 2.8 reshape.391
  380.8 4.4 copy.562
  385.2 3.0 copy.563
  397.0 3.1 copy.588
  400.1 4.5 reshape.394
  404.6 9.3 %all-to-all-start.6 = ((f32[128,1,512]{2,1,0:T(1,128)}), f32[128,1,512]{2,1,0:T(1,128)S(1)}, u32[]{:S(2)}, u32[]{:S(2)}) async-start(f32[128,1,512]{2,1,0:T(1,128)} %reshape.394), calls=%async_computation.6 | async-start | bytes 524288 | tf_op jit(solution)/shard_map/all_to_all | solution.py:224
  414.7 3.1 copy.591
  417.8 4.5 reshape.392
  422.2 5.9 %all-to-all-done.6 = f32[128,1,512]{2,1,0:T(1,128)S(1)} async-done(((f32[128,1,512]{2,1,0:T(1,128)}), f32[128,1,512]{2,1,0:T(1,128)S(1)}, u32[]{:S(2)}, u32[]{:S(2)}) %all-to-all-start.6) | async-done | bytes 262176 | tf_op jit(solution)/shard_map/all_to_all | solution.py:224
  428.2 10.4 %all-to-all-start.7 = ((f32[128,1,512]{2,1,0:T(1,128)}), f32[128,1,512]{2,1,0:T(1,128)S(1)}, u32[]{:S(2)}, u32[]{:S(2)}) async-start(f32[128,1,512]{2,1,0:T(1,128)} %reshape.392), calls=%async_computation.7 | async-start | bytes 524288 | tf_op jit(solution)/shard_map/all_to_all | solution.py:225
  438.5 16.2 %psum.21 = f32[8]{0:T(128)S(1)} all-reduce(f32[8]{0:T(128)S(1)} %get-tuple-element.14), channel_id=1, replica_groups=mesh['grp'=2,'row_0'=8,'row_1'=8,'row_2'=2] {'row_0'}, use_global_device_ids=true, to_apply=%region_1.0 | all-reduce | flops 8 | bytes 64 | tf_op jit(solution)/shard_map/psum | solution.py:16
  454.7 12.9 %psum.22 = f32[8]{0:T(128)S(1)} all-reduce(f32[8]{0:T(128)S(1)} %psum.21), channel_id=1, replica_groups=mesh['grp'=2,'row_0'=8,'row_1'=8,'row_2'=2] {'row_1'}, use_global_device_ids=true, to_apply=%region_2.0 | all-reduce | flops 8 | bytes 64 | tf_op jit(solution)/shard_map/psum | solution.py:16
  467.6 9.7 %psum.23 = f32[8]{0:T(128)S(1)} all-reduce(f32[8]{0:T(128)S(1)} %psum.22), channel_id=1, replica_groups=mesh['grp'=2,'row_0'=8,'row_1'=8,'row_2'=2] {'row_2'}, use_global_device_ids=true, to_apply=%region_3.0 | all-reduce | flops 8 | bytes 64 | tf_op jit(solution)/shard_map/psum | solution.py:16
  478.6 3.6 reshape.395
  482.2 6.6 %copy.574 = f32[8,8,128,8]{3,2,1,0:T(8,128)} copy(f32[8,8,128,8]{3,0,1,2:T(8,128)} %bitcast.953) | data formatting | bytes 524288 | tf_op jit(solution)/shard_map/all_to_all | solution.py:224
  488.8 3.6 reshape.372
  494.3 3.6 reshape.393
  497.9 6.6 %copy.577 = f32[8,8,128,8]{3,2,1,0:T(8,128)} copy(f32[8,8,128,8]{3,0,1,2:T(8,128)} %bitcast.954) | data formatting | bytes 524288 | tf_op jit(solution)/shard_map/all_to_all | solution.py:225
  504.5 3.9 reshape.374
  (220 shorter events, 139.8 us)
Async XLA Ops:
  106.9 47.6 %all-to-all-start.1 = ((f32[128,1,1024]{2,1,0:T(1,128)}), f32[128,1,1024]{2,1,0:T(1,128)S(1)}, u32[]{:S(2)}, u32[]{:S(2)}) async-start(f32[128,1,1024]{2,1,0:T(1,128)} %reshape.380), calls=%async_computation.1 | async-start | bytes 1048576 | tf_op jit(solution)/shard_map/all_to_all | solution.py:172
  154.5 27.1 %all-to-all-start = ((f32[128,1,1024]{2,1,0:T(1,128)}), f32[128,1,1024]{2,1,0:T(1,128)S(1)}, u32[]{:S(2)}, u32[]{:S(2)}) async-start(f32[128,1,1024]{2,1,0:T(1,128)} %reshape.382), calls=%async_computation | async-start | bytes 1048576 | tf_op jit(solution)/shard_map/all_to_all | solution.py:177
  219.5 30.0 %all-to-all-start.2 = ((f32[128,1,1024]{2,1,0:T(1,128)}), f32[128,1,1024]{2,1,0:T(1,128)S(1)}, u32[]{:S(2)}, u32[]{:S(2)}) async-start(f32[128,1,1024]{2,1,0:T(1,128)} %reshape.386), calls=%async_computation.2 | async-start | bytes 1048576 | tf_op jit(solution)/shard_map/all_to_all | solution.py:191
  249.4 28.4 %all-to-all-start.3 = ((f32[128,1,1024]{2,1,0:T(1,128)}), f32[128,1,1024]{2,1,0:T(1,128)S(1)}, u32[]{:S(2)}, u32[]{:S(2)}) async-start(f32[128,1,1024]{2,1,0:T(1,128)} %reshape.384), calls=%async_computation.3 | async-start | bytes 1048576 | tf_op jit(solution)/shard_map/all_to_all | solution.py:192
  285.1 16.8 %copy-start = (f32[8,8,1024]{2,1,0:T(8,128)S(1)}, f32[8,8,1024]{2,1,0:T(8,128)}, u32[]{:S(2)}) copy-start(f32[8,8,1024]{2,1,0:T(8,128)} %param.3) | copy-start | bytes 786436
  285.1 16.8 %copy-start.1 = (f32[8]{0:T(128)S(1)}, f32[8]{0:T(128)}, u32[]{:S(2)}) copy-start(f32[8]{0:T(128)} %param.5) | copy-start | bytes 100
  312.8 36.3 %all-to-all-start.5 = ((f32[128,1,1024]{2,1,0:T(1,128)}), f32[128,1,1024]{2,1,0:T(1,128)S(1)}, u32[]{:S(2)}, u32[]{:S(2)}) async-start(f32[128,1,1024]{2,1,0:T(1,128)} %reshape.388), calls=%async_computation.5 | async-start | bytes 1048576 | tf_op jit(solution)/shard_map/all_to_all | solution.py:203
  349.1 27.1 %all-to-all-start.4 = ((f32[128,1,1024]{2,1,0:T(1,128)}), f32[128,1,1024]{2,1,0:T(1,128)S(1)}, u32[]{:S(2)}, u32[]{:S(2)}) async-start(f32[128,1,1024]{2,1,0:T(1,128)} %reshape.390), calls=%async_computation.4 | async-start | bytes 1048576 | tf_op jit(solution)/shard_map/all_to_all | solution.py:204
  400.1 77.3 %copy-start.3 = (f32[8]{0:T(128)S(1)}, f32[8]{0:T(128)}, u32[]{:S(2)}) copy-start(f32[8]{0:T(128)} %param.4) | copy-start | bytes 100
  404.6 23.6 %all-to-all-start.6 = ((f32[128,1,512]{2,1,0:T(1,128)}), f32[128,1,512]{2,1,0:T(1,128)S(1)}, u32[]{:S(2)}, u32[]{:S(2)}) async-start(f32[128,1,512]{2,1,0:T(1,128)} %reshape.394), calls=%async_computation.6 | async-start | bytes 524288 | tf_op jit(solution)/shard_map/all_to_all | solution.py:224
  428.2 64.9 %all-to-all-start.7 = ((f32[128,1,512]{2,1,0:T(1,128)}), f32[128,1,512]{2,1,0:T(1,128)S(1)}, u32[]{:S(2)}, u32[]{:S(2)}) async-start(f32[128,1,512]{2,1,0:T(1,128)} %reshape.392), calls=%async_computation.7 | async-start | bytes 524288 | tf_op jit(solution)/shard_map/all_to_all | solution.py:225
  477.3 33.9 %copy-start.2 = (f32[8]{0:T(128)}, f32[8]{0:T(128)S(1)}, u32[]{:S(2)}) copy-start(f32[8]{0:T(128)S(1)} %multiply_subtract_fusion.13) | copy-start | bytes 100
